TPU v7x, 32 devices: a whole 2x2x4 slice. The times are simulated.
32 devices in a mesh: groups: 2 (over y), range: 8 (over z, x), sub: 2 (over core).
Axes of the slice: x: 2, y: 2, z: 4, core: 2. Of those that a mesh axis runs over, the one named last changes fastest.
Arguments:
- samples: float32 [2, 1024, 32, 128], P(None, ('groups', 'range', 'sub')), parts along dimension 1, may hold values from -6 to 6
- beam_weights: float32 [32, 8, 2, 64, 128], P(('groups', 'range'), None, None, None, 'sub'), parts along dimension 0, may hold values from -0.25 to 0.25
- subarrays: int32 [32, 8, 64], P(('groups', 'range', 'sub')), parts along dimension 0, may hold values from 0 to 511, as said below
- training: int32 [64], P(('groups', 'range', 'sub')), parts along dimension 0, may hold values 0 or 1
Outputs:
- covariance: float32 [32, 8, 64, 128], P(('groups', 'range', 'sub')), parts along dimension 0
- filtered: float32 [2, 128, 64, 128], P(None, None, ('groups', 'range', 'sub')), parts along dimension 2
- energy: float32 [256], P('groups'), parts along dimension 0
There are 2 independent parts, one for each index of `groups`. A program takes and returns all parts, laid end to end along the dimension named above; each array names one. Nothing has to cross between parts.
Inputs may be any that keep to these rules, and one draw needn't show every extreme that they name: `subarrays`: in each gate block the 512 indices are all 512 channels, each once.
All inputs are finite; a program needn't handle non-finite values. No bound on the sum of `training` on one device may be relied on, other than what follows from the above.
Results may differ from a plain program's by a relative error of at most 0.0003.
Values sent between devices are 32-bit elements; how exact they have to be, the bound alone decides.
A program may use at most 64 MiB of HBM per device.

v0:
```python
import jax
import jax.numpy as jnp
from jax import lax
from jax.sharding import PartitionSpec as P

GB = 2
loading = 0.05


def block_terms(snaps, chosen, weights, masked, factor):
    highest = lax.Precision.HIGHEST
    picked = jnp.take(snaps, chosen, axis=1)
    real_part = picked[0]
    imag_part = picked[1]
    real_masked = real_part * masked
    imag_masked = imag_part * masked
    cov_real = (
        jnp.einsum("snx,smx->snm", real_masked, real_part, precision=highest)
        + jnp.einsum("snx,smx->snm", imag_masked, imag_part, precision=highest)
    ) * factor
    cov_imag = (
        jnp.einsum("snx,smx->snm", imag_masked, real_part, precision=highest)
        - jnp.einsum("snx,smx->snm", real_masked, imag_part, precision=highest)
    ) * factor
    w_real = weights[:, 0]
    w_imag = weights[:, 1]
    out_real = jnp.einsum("snk,snx->kx", w_real, real_part, precision=highest) + jnp.einsum(
        "snk,snx->kx", w_imag, imag_part, precision=highest
    )
    out_imag = jnp.einsum("snk,snx->kx", w_real, imag_part, precision=highest) - jnp.einsum(
        "snk,snx->kx", w_imag, real_part, precision=highest
    )
    prod_real = jnp.einsum("snm,smk->snk", cov_real, w_real, precision=highest) - jnp.einsum(
        "snm,smk->snk", cov_imag, w_imag, precision=highest
    )
    prod_imag = jnp.einsum("snm,smk->snk", cov_real, w_imag, precision=highest) + jnp.einsum(
        "snm,smk->snk", cov_imag, w_real, precision=highest
    )
    quadratic = jnp.sum(w_real * prod_real + w_imag * prod_imag, axis=(0, 1))
    inverse = 1.0 / jnp.sqrt(quadratic + loading)
    filtered = jnp.stack([out_real * inverse[:, None], out_imag * inverse[:, None]])
    energy = jnp.sum(out_real * out_real + out_imag * out_imag, axis=1)
    covariance = jnp.concatenate([cov_real, cov_imag], axis=-1)
    return (covariance, filtered, energy)


def body(samples, beam_weights, subarrays, training):
    range_count = lax.axis_size("range")
    core_count = lax.axis_size("sub")
    parts_iq, chan_dev, all_gates, pulses = samples.shape
    gate_dev = all_gates // (range_count * core_count)
    channels = chan_dev * range_count * core_count
    blocks_dev = gate_dev // GB
    spread = samples.reshape(parts_iq, 1, 1, chan_dev, range_count, core_count, gate_dev, pulses)
    turned = lax.all_to_all(
        lax.all_to_all(spread, "range", split_axis=4, concat_axis=1, tiled=True),
        "sub",
        split_axis=5,
        concat_axis=2,
        tiled=True,
    )
    local_data = turned.reshape(parts_iq, channels, blocks_dev, GB * pulses).transpose(2, 0, 1, 3)
    mine = lax.all_to_all(beam_weights, "sub", split_axis=0, concat_axis=4, tiled=True)
    gates_on = training.astype(jnp.float32).reshape(blocks_dev, GB)
    masked = jnp.repeat(gates_on, pulses, axis=1)
    factor = 1.0 / (GB * pulses)
    covs, filts, energies = jax.vmap(block_terms, in_axes=(0, 0, 0, 0, None))(
        local_data, subarrays, mine, masked, factor
    )
    beams = filts.shape[2]
    filtered = filts.reshape(blocks_dev, parts_iq, beams, GB, pulses).transpose(1, 2, 0, 3, 4)
    filtered = filtered.reshape(parts_iq, beams, gate_dev, pulses)
    total = lax.psum(jnp.sum(energies, axis=0), ("range", "sub"))
    energy = total / (all_gates * pulses)
    return (covs, filtered, energy)


def solution(mesh):
    placed = (
        P(None, ("groups", "range", "sub"), None, None),
        P(("groups", "range"), None, None, None, "sub"),
        P(("groups", "range", "sub"), None, None),
        P(("groups", "range", "sub")),
    )
    return jax.shard_map(
        body,
        mesh=mesh,
        in_specs=placed,
        out_specs=(
            P(("groups", "range", "sub"), None, None, None),
            P(None, None, ("groups", "range", "sub"), None),
            P("groups"),
        ),
        check_vma=False,
    )
```

profile of v0, /device:TPU:0, one launch (start us, length us, event | category | flops | bytes accessed | tf_op | source)
XLA Modules:
  0.0 92.5 jit_solution(9004139148378862796)
XLA Ops:
  0.6 2.5 %reshape.157 = f32[2,1,65536]{2,1,0:T(1,128)} reshape(f32[2,8,2,64,64]{4,3,2,1,0:T(8,128)} %param.5) | data formatting | bytes 1048576
  3.2 3.5 %all-to-all-start.2 = ((f32[2,1,65536]{2,1,0:T(1,128)}), f32[2,1,65536]{2,1,0:T(1,128)S(1)}, u32[]{:S(2)}, u32[]{:S(2)}) async-start(f32[2,1,65536]{2,1,0:T(1,128)} %reshape.157), calls=%async_computation.2 | async-start | bytes 1048576 | tf_op jit(solution)/shard_map/all_to_all | solution.py:63
  6.7 1.6 %copy.24 = f32[2,1,1,32,8,2,2,128]{7,6,3,5,0,2,1,4:T(2,128)} copy(f32[2,1,1,32,8,2,2,128]{7,6,5,4,3,0,2,1:T(2,128)S(1)} %bitcast.103) | data formatting | bytes 2097152 | tf_op jit(solution)/shard_map/reshape | solution.py:54
  8.2 0.2 all-to-all-done.2
  8.4 7.4 %all-to-all-start = ((f32[2,1,1,32,8,2,2,128]{7,6,3,5,0,2,1,4:T(2,128)}), f32[2,1,1,32,8,2,2,128]{7,6,3,5,0,2,1,4:T(2,128)S(1)}, u32[]{:S(2)}, u32[]{:S(2)}) async-start(f32[2,1,1,32,8,2,2,128]{7,6,3,5,0,2,1,4:T(2,128)} %copy.24), calls=%async_computation | async-start | bytes 2097152 | tf_op jit(solution)/shard_map/all_to_all | solution.py:56
  15.9 0.5 broadcast.75
  16.4 2.3 %reduce.5 = f32[2,65536]{1,0:T(2,128)S(1)} reduce(f32[2,1,65536]{2,1,0:T(1,128)S(1)} %all-to-all-done.2, f32[]{:T(128)} %broadcast.75), dimensions={1}, to_apply=%all_to_all.44.reduce_sub_computation | reduce | bytes 1048580 | tf_op jit(solution)/shard_map/all_to_all | solution.py:63
  18.8 0.6 reshape.158
  19.4 1.9 %copy.29 = f32[1,8,2,64,2,64]{5,4,3,1,2,0:T(2,128)} copy(f32[1,8,2,64,2,64]{5,3,2,1,4,0:T(8,128)S(1)} %bitcast.98) | data formatting | bytes 1048576 | tf_op jit(solution)/shard_map/all_to_all | solution.py:63
  21.2 1.8 %all_to_all.47 = f32[1,8,2,64,128]{4,3,1,2,0:T(8,128)S(1)} reshape(f32[1,8,2,64,2,64]{5,4,3,1,2,0:T(2,128)} %copy.29) | data formatting | bytes 1048576 | tf_op jit(solution)/shard_map/all_to_all | solution.py:63
  23.1 18.9 %all-to-all-done = f32[2,1,1,32,8,2,2,128]{7,6,3,5,0,2,1,4:T(2,128)S(1)} async-done(((f32[2,1,1,32,8,2,2,128]{7,6,3,5,0,2,1,4:T(2,128)}), f32[2,1,1,32,8,2,2,128]{7,6,3,5,0,2,1,4:T(2,128)S(1)}, u32[]{:S(2)}, u32[]{:S(2)}) %all-to-all-start) | async-done | bytes 1048608 | tf_op jit(solution)/shard_map/all_to_all | solution.py:56
  42.1 4.6 %all_to_all.51 = f32[2,8,1,32,1,2,2,128]{7,6,3,1,0,4,2,5:T(2,128)S(1)} all-to-all(f32[2,8,1,32,1,2,2,128]{7,6,3,1,0,4,2,5:T(2,128)S(1)} %copy.25), channel_id=1, replica_groups=mesh['groups'=2,'range'=8,'sub'=2] {'sub'}, dimensions={5} | all-to-all | bytes 2097152 | tf_op jit(solution)/shard_map/all_to_all | solution.py:55
  46.8 0.8 copy.27
  47.6 2.3 %gather_fusion = f32[512,2,256]{2,1,0:T(2,128)S(1)} fusion(f32[1,2,512,256]{3,1,2,0:T(2,128)S(1)} %copy.27, s32[512]{0:T(512)S(1)} %reshape.147), kind=kCustom, calls=%fused_computation | custom fusion | bytes 2101248 | tf_op jit(solution)/shard_map/vmap(jit(_take))/gather | solution.py:12
  50.1 0.1 broadcast_select_fusion
  50.2 1.0 %convolution_bitcast_fusion.2 = f32[256,128]{1,0:T(8,128)S(1)} fusion(f32[1,2,8,64,256]{4,3,2,1,0:T(8,128)S(1)} %broadcast_select_fusion, f32[1,8,2,64,128]{4,3,1,2,0:T(8,128)S(1)} %all_to_all.47), kind=kOutput, calls=%fused_computation.13 | convolution fusion | flops 201326592 | bytes 917504 | tf_op jit(solution)/shard_map/vmap(snk,snx->kx)/dot_general | solution.py:27
  51.2 1.0 %convolution_bitcast_fusion = f32[256,128]{1,0:T(8,128)S(1)} fusion(f32[1,2,8,64,256]{4,3,2,1,0:T(8,128)S(1)} %broadcast_select_fusion, f32[1,8,2,64,128]{4,3,1,2,0:T(8,128)S(1)} %all_to_all.47), kind=kOutput, calls=%fused_computation.11 | convolution fusion | flops 201326592 | bytes 917504 | tf_op jit(solution)/shard_map/vmap(snk,snx->kx)/dot_general | solution.py:30
  52.2 0.6 fusion.12
  52.9 0.6 fusion.2
  53.5 0.4 fusion.19
  53.9 0.4 fusion.18
  54.3 0.6 fusion.8
  54.9 1.0 %fusion.6 = f32[256,128]{1,0:T(8,128)S(1)} fusion(f32[256,128]{1,0:T(8,128)S(1)} %convolution_bitcast_fusion.2, f32[1,2,8,64,256]{4,3,2,1,0:T(8,128)S(1)} %broadcast_select_fusion, f32[1,8,2,64,128]{4,3,1,2,0:T(8,128)S(1)} %all_to_all.47), kind=kOutput, calls=%fused_computation.15 | convolution fusion | flops 201359360 | bytes 1048576 | tf_op jit(solution)/shard_map/vmap(snk,snx->kx)/dot_general | solution.py:27
  55.9 0.6 fusion.3
  56.5 0.4 fusion
  56.9 0.4 fusion.5
  57.4 1.0 %add_reduce_fusion = (f32[128]{0:T(128)S(1)}, f32[256,128]{1,0:T(8,128)S(1)}, f32[256,128]{1,0:T(8,128)S(1)}) fusion(f32[256,128]{1,0:T(8,128)S(1)} %fusion.6, f32[128]{0:T(128)S(1)} %add_rsqrt_fusion, f32[256,128]{1,0:T(8,128)S(1)} %convolution_bitcast_fusion, f32[1,8,2,64,128]{4,3,1,2,0:T(8,128)S(1)} %all_to_all.47, ...), kind=kOutput, calls=%fused_computation.36 | convolution fusion | flops 201555840 | bytes 1311744 | tf_op jit(solution)/shard_map/vmap(snk,snx->kx)/dot_general | solution.py:30
  58.4 31.6 %psum.7 = f32[128]{0:T(128)S(1)} all-reduce(f32[128]{0:T(128)S(1)} %get-tuple-element.3), channel_id=1, replica_groups=mesh['groups'=2,'range'=8,'sub'=2] {'range','sub'}, use_global_device_ids=true, to_apply=%region_2.3 | all-reduce | flops 128 | bytes 1024 | tf_op jit(solution)/shard_map/psum | solution.py:73
  90.1 0.5 broadcast_multiply_fusion.2
  90.7 0.1 copy.31
  90.8 0.8 pad_maximum_fusion
  91.7 0.8 pad_maximum_fusion.1
  (18 shorter events, 0.5 us)
Async XLA Ops:
  0.6 6.0 %copy-start = (f32[2,32,32,128]{3,2,1,0:T(8,128)S(1)}, f32[2,32,32,128]{3,2,1,0:T(8,128)}, u32[]{:S(2)}) copy-start(f32[2,32,32,128]{3,2,1,0:T(8,128)} %param.4) | copy-start | bytes 3145732
  3.2 5.2 %all-to-all-start.2 = ((f32[2,1,65536]{2,1,0:T(1,128)}), f32[2,1,65536]{2,1,0:T(1,128)S(1)}, u32[]{:S(2)}, u32[]{:S(2)}) async-start(f32[2,1,65536]{2,1,0:T(1,128)} %reshape.157), calls=%async_computation.2 | async-start | bytes 1048576 | tf_op jit(solution)/shard_map/all_to_all | solution.py:63
  8.2 7.6 %copy-start.2 = (s32[2]{0:T(128)S(1)}, s32[2]{0:T(128)}, u32[]{:S(2)}) copy-start(s32[2]{0:T(128)} %param.7) | copy-start | bytes 28
  8.4 7.4 %copy-start.1 = (s32[1,8,64]{2,1,0:T(8,128)S(1)}, s32[1,8,64]{2,1,0:T(8,128)}, u32[]{:S(2)}) copy-start(s32[1,8,64]{2,1,0:T(8,128)} %param.6) | copy-start | bytes 6148
  8.4 33.7 %all-to-all-start = ((f32[2,1,1,32,8,2,2,128]{7,6,3,5,0,2,1,4:T(2,128)}), f32[2,1,1,32,8,2,2,128]{7,6,3,5,0,2,1,4:T(2,128)S(1)}, u32[]{:S(2)}, u32[]{:S(2)}) async-start(f32[2,1,1,32,8,2,2,128]{7,6,3,5,0,2,1,4:T(2,128)} %copy.24), calls=%async_computation | async-start | bytes 2097152 | tf_op jit(solution)/shard_map/all_to_all | solution.py:56
where the time goes:
time: 92.9 us; the launch traced here: 92.5 us
  blocking collectives  36.2 us (39%)
  waiting for transfers between devices  19.1 us (21%)
  local copies, waits for them, and re-layouts  12.7 us (14%)
  starting transfers between devices  10.9 us (12%)
  matrix products  8.13 us (9%)
  other arithmetic  4.67 us (5%)
    psum x1, blocking collectives, body(): total = lax.psum(jnp.sum(energies, axis=0), ('range', 'sub'))  31.6 us
    all_to_all x1, waiting for transfers between devices, body(): lax.all_to_all(spread, 'range', split_axis=4, concat_axis=1, tiled=True)  18.9 us
    all_to_all x1, starting transfers between devices, body(): lax.all_to_all(spread, 'range', split_axis=4, concat_axis=1, tiled=True)  7.41 us
    all_to_all x1, blocking collectives, body(): lax.all_to_all(lax.all_to_all(spread, 'range', split_axis=4, concat_axis=...  4.58 us
    all_to_all x3, local copies, waits for them, and re-layouts, body(): lax.all_to_all(beam_weights, 'sub', split_axis=0, concat_axis=4, tiled=True)  4.18 us
    all_to_all x1, starting transfers between devices, body(): lax.all_to_all(beam_weights, 'sub', split_axis=0, concat_axis=4, tiled=True)  3.49 us
    unnamed x8, local copies, waits for them, and re-layouts  3.15 us
    gather x4, local copies, waits for them, and re-layouts, block_terms(): picked = jnp.take(snaps, chosen, axis=1)  2.5 us
  transfers between devices with their start and end apart: 2, of which 2 were waited for; matrix products, arithmetic and copies ran while one was open for 8% of the time, Pallas kernels for 0%

commit v1 on v0

--- a/solution.py
+++ b/solution.py
@@ -52,12 +52,20 @@
     channels = chan_dev * range_count * core_count
     blocks_dev = gate_dev // GB
     spread = samples.reshape(parts_iq, 1, 1, chan_dev, range_count, core_count, gate_dev, pulses)
-    turned = lax.all_to_all(
-        lax.all_to_all(spread, "range", split_axis=4, concat_axis=1, tiled=True),
-        "sub",
-        split_axis=5,
-        concat_axis=2,
-        tiled=True,
+    turned = jnp.concatenate(
+        lax.all_to_all(
+            jnp.stack(
+                jnp.split(
+                    lax.all_to_all(spread, "range", split_axis=4, concat_axis=1, tiled=True),
+                    lax.axis_size("sub"),
+                    axis=5,
+                )
+            ),
+            "sub",
+            0,
+            0,
+        ),
+        axis=2,
     )
     local_data = turned.reshape(parts_iq, channels, blocks_dev, GB * pulses).transpose(2, 0, 1, 3)
     mine = lax.all_to_all(beam_weights, "sub", split_axis=0, concat_axis=4, tiled=True)

time: 92.9 us -> 93.8 us (level)
  no operation moved by 1% of the time
where the time goes in v1:
time: 93.8 us; the launch traced here: 93.4 us
  blocking collectives  36.2 us (39%)
  waiting for transfers between devices  19.1 us (20%)
  local copies, waits for them, and re-layouts  12.8 us (14%)
  starting transfers between devices  10.9 us (12%)
  matrix products  8.13 us (9%)
  other arithmetic  5.43 us (6%)
    psum x1, blocking collectives, body(): total = lax.psum(jnp.sum(energies, axis=0), ('range', 'sub'))  31.6 us
    all_to_all x1, waiting for transfers between devices, body(): lax.all_to_all(spread, 'range', split_axis=4, concat_axis=1, tiled=True)  18.9 us
    all_to_all x1, starting transfers between devices, body(): lax.all_to_all(spread, 'range', split_axis=4, concat_axis=1, tiled=True)  7.41 us
    all_to_all x1, blocking collectives, body(): lax.all_to_all(jnp.stack(jnp.split(lax.all_to_all(spread, 'range', split_...  4.58 us
    all_to_all x3, local copies, waits for them, and re-layouts, body(): lax.all_to_all(beam_weights, 'sub', split_axis=0, concat_axis=4, tiled=True)  4.18 us
    all_to_all x1, starting transfers between devices, body(): lax.all_to_all(beam_weights, 'sub', split_axis=0, concat_axis=4, tiled=True)  3.49 us
    unnamed x8, local copies, waits for them, and re-layouts  3.15 us
    gather x4, local copies, waits for them, and re-layouts, block_terms(): picked = jnp.take(snaps, chosen, axis=1)  2.5 us
  transfers between devices with their start and end apart: 2, of which 2 were waited for; matrix products, arithmetic and copies ran while one was open for 8% of the time, Pallas kernels for 0%

profile of v1, /device:TPU:0, one launch (start us, length us, event | category | flops | bytes accessed | tf_op | source)
XLA Modules:
  0.0 93.4 jit_solution(11681672451801026995)
XLA Ops:
  0.6 2.5 %reshape.160 = f32[2,1,65536]{2,1,0:T(1,128)} reshape(f32[2,8,2,64,64]{4,3,2,1,0:T(8,128)} %param.5) | data formatting | bytes 1048576
  3.2 3.5 %all-to-all-start.2 = ((f32[2,1,65536]{2,1,0:T(1,128)}), f32[2,1,65536]{2,1,0:T(1,128)S(1)}, u32[]{:S(2)}, u32[]{:S(2)}) async-start(f32[2,1,65536]{2,1,0:T(1,128)} %reshape.160), calls=%async_computation.2 | async-start | bytes 1048576 | tf_op jit(solution)/shard_map/all_to_all | solution.py:71
  6.7 1.6 %copy.27 = f32[2,1,1,32,8,2,2,128]{7,6,3,0,5,2,1,4:T(2,128)} copy(f32[2,1,1,32,8,2,2,128]{7,6,5,4,3,0,2,1:T(2,128)S(1)} %bitcast.107) | data formatting | bytes 2097152 | tf_op jit(solution)/shard_map/reshape | solution.py:54
  8.2 0.1 all-to-all-done.2
  8.4 7.4 %all-to-all-start = ((f32[2,1,1,32,8,2,2,128]{7,6,3,0,5,2,1,4:T(2,128)}), f32[2,1,1,32,8,2,2,128]{7,6,3,0,5,2,1,4:T(2,128)S(1)}, u32[]{:S(2)}, u32[]{:S(2)}) async-start(f32[2,1,1,32,8,2,2,128]{7,6,3,0,5,2,1,4:T(2,128)} %copy.27), calls=%async_computation | async-start | bytes 2097152 | tf_op jit(solution)/shard_map/all_to_all | solution.py:59
  15.9 0.5 broadcast.75
  16.4 2.3 %reduce.5 = f32[2,65536]{1,0:T(2,128)S(1)} reduce(f32[2,1,65536]{2,1,0:T(1,128)S(1)} %all-to-all-done.2, f32[]{:T(128)} %broadcast.75), dimensions={1}, to_apply=%all_to_all.34.reduce_sub_computation | reduce | bytes 1048580 | tf_op jit(solution)/shard_map/all_to_all | solution.py:71
  18.8 0.6 reshape.161
  19.4 1.9 %copy.33 = f32[1,8,2,64,2,64]{5,4,3,1,2,0:T(2,128)} copy(f32[1,8,2,64,2,64]{5,3,2,1,4,0:T(8,128)S(1)} %bitcast.102) | data formatting | bytes 1048576 | tf_op jit(solution)/shard_map/all_to_all | solution.py:71
  21.2 1.8 %all_to_all.37 = f32[1,8,2,64,128]{4,3,1,2,0:T(8,128)S(1)} reshape(f32[1,8,2,64,2,64]{5,4,3,1,2,0:T(2,128)} %copy.33) | data formatting | bytes 1048576 | tf_op jit(solution)/shard_map/all_to_all | solution.py:71
  23.1 18.9 %all-to-all-done = f32[2,1,1,32,8,2,2,128]{7,6,3,0,5,2,1,4:T(2,128)S(1)} async-done(((f32[2,1,1,32,8,2,2,128]{7,6,3,0,5,2,1,4:T(2,128)}), f32[2,1,1,32,8,2,2,128]{7,6,3,0,5,2,1,4:T(2,128)S(1)}, u32[]{:S(2)}, u32[]{:S(2)}) %all-to-all-start) | async-done | bytes 1048608 | tf_op jit(solution)/shard_map/all_to_all | solution.py:59
  42.1 0.8 pad_maximum_fusion
  43.0 4.6 %all_to_all.41 = f32[2,2,8,1,32,1,1,2,128]{8,7,3,4,2,1,6,5,0:T(2,128)S(1)} all-to-all(f32[2,2,8,1,32,1,1,2,128]{8,7,3,4,2,1,6,5,0:T(2,128)S(1)} %copy.29), channel_id=1, replica_groups=mesh['groups'=2,'range'=8,'sub'=2] {'sub'}, dimensions={0} | all-to-all | bytes 2097152 | tf_op jit(solution)/shard_map/all_to_all | solution.py:56
  47.7 0.8 copy.31
  48.5 2.3 %gather_fusion = f32[512,2,256]{2,1,0:T(2,128)S(1)} fusion(f32[1,2,512,256]{3,1,2,0:T(2,128)S(1)} %copy.31, s32[512]{0:T(512)S(1)} %reshape.150), kind=kCustom, calls=%fused_computation | custom fusion | bytes 2101248 | tf_op jit(solution)/shard_map/vmap(jit(_take))/gather | solution.py:12
  51.0 0.1 broadcast_select_fusion
  51.1 1.0 %convolution_bitcast_fusion.2 = f32[256,128]{1,0:T(8,128)S(1)} fusion(f32[1,2,8,64,256]{4,3,2,1,0:T(8,128)S(1)} %broadcast_select_fusion, f32[1,8,2,64,128]{4,3,1,2,0:T(8,128)S(1)} %all_to_all.37), kind=kOutput, calls=%fused_computation.13 | convolution fusion | flops 201326592 | bytes 917504 | tf_op jit(solution)/shard_map/vmap(snk,snx->kx)/dot_general | solution.py:27
  52.1 1.0 %convolution_bitcast_fusion = f32[256,128]{1,0:T(8,128)S(1)} fusion(f32[1,2,8,64,256]{4,3,2,1,0:T(8,128)S(1)} %broadcast_select_fusion, f32[1,8,2,64,128]{4,3,1,2,0:T(8,128)S(1)} %all_to_all.37), kind=kOutput, calls=%fused_computation.11 | convolution fusion | flops 201326592 | bytes 917504 | tf_op jit(solution)/shard_map/vmap(snk,snx->kx)/dot_general | solution.py:30
  53.1 0.6 fusion.12
  53.7 0.6 fusion.2
  54.4 0.4 fusion.19
  54.8 0.4 fusion.18
  55.2 0.6 fusion.8
  55.8 1.0 %fusion.6 = f32[256,128]{1,0:T(8,128)S(1)} fusion(f32[256,128]{1,0:T(8,128)S(1)} %convolution_bitcast_fusion.2, f32[1,2,8,64,256]{4,3,2,1,0:T(8,128)S(1)} %broadcast_select_fusion, f32[1,8,2,64,128]{4,3,1,2,0:T(8,128)S(1)} %all_to_all.37), kind=kOutput, calls=%fused_computation.15 | convolution fusion | flops 201359360 | bytes 1048576 | tf_op jit(solution)/shard_map/vmap(snk,snx->kx)/dot_general | solution.py:27
  56.8 0.6 fusion.3
  57.4 0.4 fusion
  57.8 0.4 fusion.5
  58.3 1.0 %add_reduce_fusion = (f32[128]{0:T(128)S(1)}, f32[256,128]{1,0:T(8,128)S(1)}, f32[256,128]{1,0:T(8,128)S(1)}) fusion(f32[256,128]{1,0:T(8,128)S(1)} %fusion.6, f32[128]{0:T(128)S(1)} %add_rsqrt_fusion, f32[256,128]{1,0:T(8,128)S(1)} %convolution_bitcast_fusion, f32[1,8,2,64,128]{4,3,1,2,0:T(8,128)S(1)} %all_to_all.37, ...), kind=kOutput, calls=%fused_computation.39 | convolution fusion | flops 201555840 | bytes 1311744 | tf_op jit(solution)/shard_map/vmap(snk,snx->kx)/dot_general | solution.py:30
  59.3 31.6 %psum.7 = f32[128]{0:T(128)S(1)} all-reduce(f32[128]{0:T(128)S(1)} %get-tuple-element.5), channel_id=1, replica_groups=mesh['groups'=2,'range'=8,'sub'=2] {'range','sub'}, use_global_device_ids=true, to_apply=%region_2.3 | all-reduce | flops 128 | bytes 1024 | tf_op jit(solution)/shard_map/psum | solution.py:81
  90.9 0.5 broadcast_multiply_fusion.2
  91.7 0.8 pad_maximum_fusion.1
  92.5 0.8 pad_maximum_fusion.2
  (20 shorter events, 0.8 us)
Async XLA Ops:
  0.6 6.0 %copy-start = (f32[2,32,32,128]{3,2,1,0:T(8,128)S(1)}, f32[2,32,32,128]{3,2,1,0:T(8,128)}, u32[]{:S(2)}) copy-start(f32[2,32,32,128]{3,2,1,0:T(8,128)} %param.4) | copy-start | bytes 3145732
  3.2 5.2 %all-to-all-start.2 = ((f32[2,1,65536]{2,1,0:T(1,128)}), f32[2,1,65536]{2,1,0:T(1,128)S(1)}, u32[]{:S(2)}, u32[]{:S(2)}) async-start(f32[2,1,65536]{2,1,0:T(1,128)} %reshape.160), calls=%async_computation.2 | async-start | bytes 1048576 | tf_op jit(solution)/shard_map/all_to_all | solution.py:71
  8.2 7.6 %copy-start.2 = (s32[2]{0:T(128)S(1)}, s32[2]{0:T(128)}, u32[]{:S(2)}) copy-start(s32[2]{0:T(128)} %param.7) | copy-start | bytes 28
  8.4 7.4 %copy-start.1 = (s32[1,8,64]{2,1,0:T(8,128)S(1)}, s32[1,8,64]{2,1,0:T(8,128)}, u32[]{:S(2)}) copy-start(s32[1,8,64]{2,1,0:T(8,128)} %param.6) | copy-start | bytes 6148
  8.4 33.7 %all-to-all-start = ((f32[2,1,1,32,8,2,2,128]{7,6,3,0,5,2,1,4:T(2,128)}), f32[2,1,1,32,8,2,2,128]{7,6,3,0,5,2,1,4:T(2,128)S(1)}, u32[]{:S(2)}, u32[]{:S(2)}) async-start(f32[2,1,1,32,8,2,2,128]{7,6,3,0,5,2,1,4:T(2,128)} %copy.27), calls=%async_computation | async-start | bytes 2097152 | tf_op jit(solution)/shard_map/all_to_all | solution.py:59
